TPU v7x, 32 devices: a whole 2x2x4 slice. The times are simulated.
32 devices in a mesh: row: 8 (over z, y), col: 2 (over core), depth: 2 (over x).
Axes of the slice: x: 2, y: 2, z: 4, core: 2. Of those that a mesh axis runs over, the one named last changes fastest.
Arguments:
- student_hidden: bfloat16 [2048, 768], P('row', ('depth', 'col')), may hold values from -16 to 16
- embedding: bfloat16 [50304, 768], P('col', ('depth', 'row')), as said below
- teacher_logits: bfloat16 [2048, 50304], P('row', ('col', 'depth')), may hold values from -24 to 124, as said below
Outputs:
- loss: float32 [2048], P('row')
- peak_logprob: float32 [2048], P('row')
Inputs may be any that keep to these rules, and one draw needn't show every extreme that they name: embedding entries lie within plus or minus 4 / sqrt(768). teacher_logits lie within -24 and 124; each token's logits carry an offset of 0 to 100.
All inputs are finite; a program needn't handle non-finite values.
Results may differ from a plain program's by a relative error of at most 0.0003.
Values may be sent and summed in bfloat16 or wider, within the bound.
A program may use at most 128 MiB of HBM per device.

v0:
```python
import jax
import jax.numpy as jnp
from jax import lax
from jax.sharding import PartitionSpec as P


def row_terms(student, teacher_values, student_peak, teacher_peak):
    weights = jnp.exp(teacher_values - teacher_peak[:, None])
    student_sum = jnp.sum(jnp.exp(student - student_peak[:, None]), axis=1)
    teacher_sum = jnp.sum(weights, axis=1)
    cross_sum = jnp.sum(weights * student, axis=1)
    return (student_sum, teacher_sum, cross_sum)


def on_device(student_hidden, embedding, teacher_logits):
    hidden_layer = lax.all_gather(student_hidden, "col", axis=1, tiled=True)
    token_count = hidden_layer.shape[0]
    hidden_full = lax.all_gather(hidden_layer, "depth", axis=1, tiled=True)
    row_count = lax.axis_size("row")
    depth_count = lax.axis_size("depth")
    narrow = embedding.shape[1]
    hidden_order = hidden_full.reshape(token_count, depth_count, row_count, narrow)
    hidden_order = hidden_order.transpose(0, 2, 1, 3).reshape(
        token_count, row_count * depth_count * narrow
    )
    vocab_rows = lax.all_to_all(embedding, "depth", split_axis=0, concat_axis=1, tiled=True)
    full_rows = lax.all_gather(vocab_rows, "row", axis=1, tiled=True)
    student = jnp.einsum("td,vd->tv", hidden_order, full_rows, preferred_element_type=jnp.float32)
    teacher_values = teacher_logits.astype(jnp.float32)
    student_top = jnp.max(student, axis=1)
    teacher_top = jnp.max(teacher_values, axis=1)
    student_peak, teacher_peak = lax.pmax((student_top, teacher_top), ("col", "depth"))
    local_student, local_teacher, local_cross = row_terms(
        student, teacher_values, student_peak, teacher_peak
    )
    student_sum, teacher_sum, cross_sum = lax.psum(
        (local_student, local_teacher, local_cross), ("col", "depth")
    )
    norm_log = jnp.log(student_sum)
    loss = student_peak + norm_log - cross_sum / teacher_sum
    return (loss, -norm_log)


def solution(mesh):
    in_specs = (P("row", ("depth", "col")), P("col", ("depth", "row")), P("row", ("col", "depth")))
    out_specs = (P("row"), P("row"))
    return jax.shard_map(
        on_device, mesh=mesh, in_specs=in_specs, out_specs=out_specs, check_vma=False
    )
```

profile of v0, /device:TPU:0, one launch (start us, length us, event | category | flops | bytes accessed | tf_op | source)
XLA Modules:
  0.0 464.3 jit_solution(10611060444776623536)
XLA Ops:
  7.2 0.0 copy-start
  7.2 0.0 all-gather.2.cloned.1.call-start
  7.2 3.9 all_to_all.14
  11.1 0.2 copy.8
  11.4 33.4 %all_to_all.19 = bf16[2,12576,48]{1,2,0:T(8,128)(2,1)} all-to-all(bf16[2,12576,48]{1,2,0:T(8,128)(2,1)S(1)} %copy.8), channel_id=1, replica_groups=mesh['row'=8,'col'=2,'depth'=2] {'depth'}, dimensions={0} | all-to-all | bytes 4829184 | tf_op jit(solution)/shard_map/all_to_all | solution.py:26
  44.8 0.0 all-gather.2.cloned.1.call-update
  44.8 0.0 copy-done
  44.8 1.9 all_gather.9
  46.8 7.6 %all_gather.10 = bf16[256,768]{0,1:T(8,128)(2,1)S(1)} all-gather(bf16[256,384]{0,1:T(8,128)(2,1)S(1)} %all_gather.9), channel_id=1, replica_groups=mesh['row'=8,'col'=2,'depth'=2] {'depth'}, dimensions={1}, use_global_device_ids=true | all-gather | bytes 589824 | tf_op jit(solution)/shard_map/all_gather | solution.py:18
  54.4 4.4 reduce_max.24
  58.8 360.2 %all-gather.2.cloned.1.call-done = bf16[12576,768]{0,1:T(8,128)(2,1)} async-done(((bf16[12576,96]{0,1:T(8,128)(2,1)}), bf16[12576,768]{0,1:T(8,128)(2,1)}) %all-gather.2.cloned.1.call-update) | async-done | bytes 19316752 | tf_op jit(solution)/shard_map/all_gather | solution.py:27
  419.0 14.5 %fusion.1 = (f32[256]{0:T(256)S(1)}, f32[256,12576]{0,1:T(8,128)}) fusion(bf16[256,768]{0,1:T(8,128)(2,1)S(1)} %bitcast.12, bf16[12576,768]{0,1:T(8,128)(2,1)} %all-gather.2.cloned.1.call-done), kind=kOutput, calls=%fused_computation.6 | convolution fusion | flops 4948303872 | bytes 32588800 | tf_op jit(solution)/shard_map/td,vd->tv/dot_general | solution.py:28
  433.5 7.4 %all-reduce.1 = (f32[256]{0:T(256)S(1)}, f32[256]{0:T(256)S(1)}) all-reduce(f32[256]{0:T(256)S(1)} %get-tuple-element.12, bf16[256]{0:T(256)(128)(2,1)S(1)} %reduce_max.24), channel_id=1, replica_groups=mesh['row'=8,'col'=2,'depth'=2] {'col','depth'}, use_global_device_ids=true, to_apply=%region_1.0 | all-reduce | flops 512 | bytes 3584 | tf_op jit(solution)/shard_map/pmax | solution.py:32
  440.9 8.9 %exponential_reduce_fusion = (f32[256]{0:T(256)S(1)}, f32[256]{0:T(256)S(1)}, f32[256]{0:T(256)S(1)}) fusion(f32[256,12576]{0,1:T(8,128)} %get-tuple-element.13, f32[256]{0:T(256)S(1)} %get-tuple-element.8, f32[256]{0:T(256)S(1)} %get-tuple-element.9, bf16[256,12576]{0,1:T(8,128)(2,1)} %param.5), kind=kLoop, calls=%fused_computation.3 | loop fusion | flops 22535424 | bytes 19321856 | tf_op jit(solution)/shard_map/reduce_sum | solution.py:9
  449.8 7.1 %all-reduce = (f32[256]{0:T(256)S(1)}, f32[256]{0:T(256)S(1)}, f32[256]{0:T(256)S(1)}) all-reduce(f32[256]{0:T(256)S(1)} %get-tuple-element.3, f32[256]{0:T(256)S(1)} %get-tuple-element.4, f32[256]{0:T(256)S(1)} %get-tuple-element.2), channel_id=1, replica_groups=mesh['row'=8,'col'=2,'depth'=2] {'col','depth'}, use_global_device_ids=true, to_apply=%region_7.0 | all-reduce | flops 768 | bytes 6144 | tf_op jit(solution)/shard_map/psum | solution.py:36
  456.9 0.6 log_negate_fusion
  (1 shorter events, 0.0 us)
Async XLA Ops:
  7.2 37.7 %copy-start = (bf16[256,192]{0,1:T(8,128)(2,1)S(1)}, bf16[256,192]{0,1:T(8,128)(2,1)}, u32[]{:S(2)}) copy-start(bf16[256,192]{0,1:T(8,128)(2,1)} %param.3) | copy-start | bytes 294916
  7.2 411.8 %all-gather.2.cloned.1.call-start = ((), (), s32[]{:S(2)}) async-start(), calls=%async_computation.1 | async-start | bytes 21897216 | tf_op jit(solution)/shard_map/all_gather | solution.py:27
Sparse Core Ops, SparseCore 0:
  44.9 374.0 all-gather.1
where the time goes:
time: 465 us; the launch traced here: 464 us
  waiting for transfers between devices  360 us (77%)
  blocking collectives  57.5 us (12%)
  matrix products  14.5 us (3%)
  between operations  14.1 us (3%)
  other arithmetic  13.8 us (3%)
    all_gather x1, waiting for transfers between devices, on_device(): full_rows = lax.all_gather(vocab_rows, 'row', axis=1, tiled=True)  360 us
    all_to_all x1, blocking collectives, on_device(): lax.all_to_all(embedding, 'depth', split_axis=0, concat_axis=1, tiled=True)  33.4 us
    dot_general x1, matrix products, on_device(): jnp.einsum('td,vd->tv', hidden_order, full_rows, preferred_element_type=j...  14.5 us
  transfers between devices with their start and end apart: 1, of which 1 were waited for; matrix products, arithmetic and copies ran while one was open for 1% of the time, Pallas kernels for 0%

commit v1 on v0

--- a/solution.py
+++ b/solution.py
@@ -24,7 +24,9 @@
         token_count, row_count * depth_count * narrow
     )
     vocab_rows = lax.all_to_all(embedding, "depth", split_axis=0, concat_axis=1, tiled=True)
-    full_rows = lax.all_gather(vocab_rows, "row", axis=1, tiled=True)
+    full_rows = jnp.concatenate(
+        lax.all_to_all(jnp.stack([vocab_rows] * lax.axis_size("row")), "row", 0, 0), axis=1
+    )
     student = jnp.einsum("td,vd->tv", hidden_order, full_rows, preferred_element_type=jnp.float32)
     teacher_values = teacher_logits.astype(jnp.float32)
     student_top = jnp.max(student, axis=1)

time: 465 us -> 509 us (1.095)
  waiting for transfers between devices: 360 us -> 406 us
  between operations: 14.1 us -> 0.66 us
  local copies, waits for them, and re-layouts: 4.17 us -> 11.1 us
  starting transfers between devices: 0.04 us -> 6.21 us
    all_to_all x0 -> x1, waiting for transfers between devices: none -> 406 us  [on_device(): lax.all_to_all(jnp.stack([vocab_rows] * lax.axis_size('row')), 'row', 0, 0)]
    all_gather x1 -> x0, waiting for transfers between devices: 360 us -> none  [on_device(): full_rows = lax.all_gather(vocab_rows, 'row', axis=1, tiled=True)]
    another operation x0 -> x1, local copies, waits for them, and re-layouts: none -> 6.95 us  [on_device(): jnp.stack([vocab_rows] * lax.axis_size('row'))]
    all_to_all x0 -> x1, starting transfers between devices: none -> 6.21 us  [on_device(): lax.all_to_all(jnp.stack([vocab_rows] * lax.axis_size('row')), 'row', 0, 0)]
where the time goes in v1:
time: 509 us
  waiting for transfers between devices  406 us (80%)
  blocking collectives  56.5 us (11%)
  matrix products  14.5 us (3%)
  other arithmetic  13.8 us (3%)
  local copies, waits for them, and re-layouts  11.1 us (2%)
  starting transfers between devices  6.21 us (1%)
    all_to_all x1, waiting for transfers between devices, on_device(): lax.all_to_all(jnp.stack([vocab_rows] * lax.axis_size('row')), 'row', 0, 0)  406 us
    all_to_all x1, blocking collectives, on_device(): lax.all_to_all(embedding, 'depth', split_axis=0, concat_axis=1, tiled=True)  32.5 us
    dot_general x1, matrix products, on_device(): jnp.einsum('td,vd->tv', hidden_order, full_rows, preferred_element_type=j...  14.5 us
  transfers between devices with their start and end apart: 1, of which 1 were waited for; matrix products, arithmetic and copies ran while one was open for 1% of the time, Pallas kernels for 0%

profile of v1, /device:TPU:0, one launch (start us, length us, event | category | flops | bytes accessed | tf_op | source)
XLA Modules:
  0.0 508.9 jit_solution(8812044764522152691)
XLA Ops:
  0.6 3.9 all_to_all.15
  4.5 0.2 copy.8
  4.8 32.5 %all_to_all.21 = bf16[2,12576,48]{1,2,0:T(8,128)(2,1)S(1)} all-to-all(bf16[2,12576,48]{1,2,0:T(8,128)(2,1)S(1)} %copy.8), channel_id=1, replica_groups=mesh['row'=8,'col'=2,'depth'=2] {'depth'}, dimensions={0} | all-to-all | bytes 4829184 | tf_op jit(solution)/shard_map/all_to_all | solution.py:26
  37.3 6.9 %stack.5 = bf16[8,12576,96]{1,2,0:T(8,128)(2,1)} broadcast(bf16[12576,96]{0,1:T(8,128)(2,1)S(1)} %bitcast.14), dimensions={1,2} | broadcast | bytes 21731328 | tf_op jit(solution)/shard_map/stack | solution.py:28
  44.2 0.0 copy-start
  44.2 6.2 %all-to-all-start.1 = ((bf16[8,12576,96]{1,2,0:T(8,128)(2,1)}), bf16[8,12576,96]{1,2,0:T(8,128)(2,1)}, u32[]{:S(2)}, u32[]{:S(2)}) async-start(bf16[8,12576,96]{1,2,0:T(8,128)(2,1)} %stack.5), calls=%async_computation.1 | async-start | bytes 38928384 | tf_op jit(solution)/shard_map/all_to_all | solution.py:28
  50.4 0.0 copy-done
  50.4 1.9 all_gather.6
  52.4 7.6 %all_gather.7 = bf16[256,768]{0,1:T(8,128)(2,1)S(1)} all-gather(bf16[256,384]{0,1:T(8,128)(2,1)S(1)} %all_gather.6), channel_id=1, replica_groups=mesh['row'=8,'col'=2,'depth'=2] {'depth'}, dimensions={1}, use_global_device_ids=true | all-gather | bytes 589824 | tf_op jit(solution)/shard_map/all_gather | solution.py:18
  60.0 4.4 reduce_max.24
  64.4 406.1 %all-to-all-done.1 = bf16[8,12576,96]{1,2,0:T(8,128)(2,1)} async-done(((bf16[8,12576,96]{1,2,0:T(8,128)(2,1)}), bf16[8,12576,96]{1,2,0:T(8,128)(2,1)}, u32[]{:S(2)}, u32[]{:S(2)}) %all-to-all-start.1) | async-done | bytes 19316768 | tf_op jit(solution)/shard_map/all_to_all | solution.py:28
  470.5 14.5 %fusion.1 = (f32[256]{0:T(256)S(1)}, f32[256,12576]{0,1:T(8,128)}) fusion(bf16[256,768]{0,1:T(8,128)(2,1)S(1)} %bitcast.15, bf16[12576,768]{0,1:T(8,128)(2,1)} %bitcast.6), kind=kOutput, calls=%fused_computation.6 | convolution fusion | flops 4948303872 | bytes 32588800 | tf_op jit(solution)/shard_map/td,vd->tv/dot_general | solution.py:30
  485.0 6.5 %all-reduce.1 = (f32[256]{0:T(256)S(1)}, f32[256]{0:T(256)S(1)}) all-reduce(f32[256]{0:T(256)S(1)} %get-tuple-element.12, bf16[256]{0:T(256)(128)(2,1)S(1)} %reduce_max.24), channel_id=1, replica_groups=mesh['row'=8,'col'=2,'depth'=2] {'col','depth'}, use_global_device_ids=true, to_apply=%region_1.0 | all-reduce | flops 512 | bytes 3584 | tf_op jit(solution)/shard_map/pmax | solution.py:34
  491.5 8.9 %exponential_reduce_fusion = (f32[256]{0:T(256)S(1)}, f32[256]{0:T(256)S(1)}, f32[256]{0:T(256)S(1)}) fusion(f32[256,12576]{0,1:T(8,128)} %get-tuple-element.13, f32[256]{0:T(256)S(1)} %get-tuple-element.8, f32[256]{0:T(256)S(1)} %get-tuple-element.9, bf16[256,12576]{0,1:T(8,128)(2,1)} %param.5), kind=kLoop, calls=%fused_computation.3 | loop fusion | flops 22535424 | bytes 19321856 | tf_op jit(solution)/shard_map/reduce_sum | solution.py:9
  500.4 8.0 %all-reduce = (f32[256]{0:T(256)S(1)}, f32[256]{0:T(256)S(1)}, f32[256]{0:T(256)S(1)}) all-reduce(f32[256]{0:T(256)S(1)} %get-tuple-element.3, f32[256]{0:T(256)S(1)} %get-tuple-element.4, f32[256]{0:T(256)S(1)} %get-tuple-element.2), channel_id=1, replica_groups=mesh['row'=8,'col'=2,'depth'=2] {'col','depth'}, use_global_device_ids=true, to_apply=%region_7.0 | all-reduce | flops 768 | bytes 6144 | tf_op jit(solution)/shard_map/psum | solution.py:38
  508.4 0.6 log_negate_fusion
  (1 shorter events, 0.0 us)
Async XLA Ops:
  44.2 6.2 %copy-start = (bf16[256,192]{0,1:T(8,128)(2,1)S(1)}, bf16[256,192]{0,1:T(8,128)(2,1)}, u32[]{:S(2)}) copy-start(bf16[256,192]{0,1:T(8,128)(2,1)} %param.3) | copy-start | bytes 294916
  44.2 426.3 %all-to-all-start.1 = ((bf16[8,12576,96]{1,2,0:T(8,128)(2,1)}), bf16[8,12576,96]{1,2,0:T(8,128)(2,1)}, u32[]{:S(2)}, u32[]{:S(2)}) async-start(bf16[8,12576,96]{1,2,0:T(8,128)(2,1)} %stack.5), calls=%async_computation.1 | async-start | bytes 38928384 | tf_op jit(solution)/shard_map/all_to_all | solution.py:28
